TPU v7x, 256 devices: a 8x8x2 block of a 8x8x16 slice. The times are simulated.
256 devices in a mesh: scene: 2 (over z), view: 128 (over y, x, core).
Axes of the slice: x: 8, y: 8, z: 2, core: 2. Of those that a mesh axis runs over, the one named last changes fastest.
The devices are a block of a 8x8x16 slice.
Arguments:
- latents: bfloat16 [2048, 64, 512], P(('scene', 'view')), parts along dimension 0, may hold values from -48 to 48
- norm_gain: float32 [512], replicated, may hold values from 0.1 to 1.9
- norm_shift: float32 [512], replicated, may hold values from -3 to 3
- w_first: bfloat16 [512, 3, 3, 512], replicated, may hold values from -0.09375 to 0.09375
- bias_first: float32 [512], replicated, may hold values from -3 to 3
- w_second: bfloat16 [512, 3, 3, 512], replicated, may hold values from -0.09375 to 0.09375
- bias_second: float32 [512], replicated, may hold values from -3 to 3
Outputs:
- decoded: bfloat16 [4096, 128, 512], P(('scene', 'view')), parts along dimension 0
There are 2 independent parts, one for each index of `scene`. A program takes and returns all parts, laid end to end along the dimension named above; an argument that names none is the same for every part. Nothing has to cross between parts.
All inputs are finite; a program needn't handle non-finite values.
Results may differ from a plain program's by a relative error of at most 0.0051.
Values may be sent and summed in bfloat16 or wider, within the bound.
A program may use at most 128 MiB of HBM per device.

v0:
```python
import jax
import jax.numpy as jnp
from jax import lax
from jax.sharding import Mesh
from jax.sharding import PartitionSpec as P

GROUPS = 32
H_LAT = 32
VIEW = ("view_0", "view_1", "view_2")
SCENE_VIEW = ("scene", "view_0", "view_1", "view_2")
epsilon = 1e-06


def one_axis_at_a_time(array, axes):
    for axis in axes:
        array = lax.psum(array, axis)
    return array


def shifted(block, axis, distance):
    devices = range(lax.axis_size(axis))
    route = [(i - distance, i) for i in devices if i - distance in devices]
    return lax.ppermute(block, axis, route)


def conv_taps(padded, filters, out_rows, out_cols):
    result = None
    for tap_row in range(3):
        for tap_col in range(3):
            window = padded[tap_row : tap_row + out_rows, tap_col : tap_col + out_cols, :]
            term = jnp.einsum(
                "rwi,oi->rwo",
                window,
                filters[:, tap_row, tap_col, :],
                preferred_element_type=jnp.float32,
            )
            result = term if result is None else result + term
    return result


def pad_columns(block):
    return jnp.pad(block, ((0, 0), (1, 1), (0, 0)))


def keep_inside(block, first_row):
    position = first_row + jnp.arange(block.shape[0], dtype=jnp.int32)
    inside = (position >= 0) & (position < H_LAT)
    return jnp.where(inside[:, None, None], block, jnp.zeros((), block.dtype))


def spread_channels(group_values, channels):
    return jnp.broadcast_to(group_values[:, None], (GROUPS, channels // GROUPS)).reshape(channels)


def group_total(channel_values, channels):
    return jnp.sum(channel_values.reshape(GROUPS, channels // GROUPS), axis=1)


def per_device(latents, norm_gain, norm_shift, w_first, bias_first, w_second, bias_second):
    slab_rows, columns, channels = latents.shape
    slab_count = H_LAT // slab_rows
    view_count = lax.axis_size(VIEW) // slab_count
    slab_index = lax.axis_index(VIEW) // view_count
    slab_start = slab_index * slab_rows
    entries = float(slab_rows * columns * (channels // GROUPS) * lax.axis_size(VIEW))
    values = latents.astype(jnp.float32)
    group_sums = group_total(jnp.sum(values, axis=(0, 1)), channels)
    group_squares = group_total(jnp.sum(values * values, axis=(0, 1)), channels)
    total_sums, total_squares = (
        one_axis_at_a_time(group_sums, VIEW),
        one_axis_at_a_time(group_squares, VIEW),
    )
    group_mean = total_sums / entries
    group_var = total_squares / entries - group_mean * group_mean
    channel_scale = spread_channels(lax.rsqrt(group_var + epsilon), channels) * norm_gain
    channel_offset = norm_shift - spread_channels(group_mean, channels) * channel_scale
    above = shifted(latents[-2:], VIEW, view_count)
    below = shifted(latents[:2], VIEW, -view_count)
    deeper = jnp.concatenate([above, latents, below], axis=0)
    active = keep_inside(
        jax.nn.silu(deeper.astype(jnp.float32) * channel_scale + channel_offset).astype(
            jnp.bfloat16
        ),
        slab_start - 2,
    )
    filtered = conv_taps(pad_columns(active), w_first, slab_rows + 2, columns)
    mixed = (deeper[1:-1].astype(jnp.float32) + filtered + bias_first).astype(jnp.bfloat16)
    mixed = keep_inside(mixed, slab_start - 1)
    tall_rows = mixed.shape[0]
    doubled = jnp.broadcast_to(mixed[:, None, :, None, :], (tall_rows, 2, columns, 2, channels))
    doubled = doubled.reshape(2 * tall_rows, 2 * columns, channels)
    doubled = doubled[1 : 2 * slab_rows + 3]
    decoded = conv_taps(pad_columns(doubled), w_second, 2 * slab_rows, 2 * columns) + bias_second
    return decoded.astype(jnp.bfloat16)


def solution(mesh):
    torus = Mesh(
        mesh.devices.reshape(mesh.shape["scene"], 8, 8, 2), ("scene", "view_0", "view_1", "view_2")
    )
    in_specs = (P(SCENE_VIEW, None, None), P(), P(), P(), P(), P(), P())
    out_specs = P(SCENE_VIEW, None, None)
    return jax.shard_map(
        per_device, mesh=torus, in_specs=in_specs, out_specs=out_specs, check_vma=False
    )
```

profile of v0, /device:TPU:513, one launch (start us, length us, event | category | flops | bytes accessed | tf_op | source)
XLA Modules:
  0.0 123.4 jit_solution(8595949860446383407)
XLA Ops:
  0.0 1.0 fusion.96
  1.0 1.3 %collective-permute-start.1 = (bf16[2,64,512]{2,1,0:T(8,128)(2,1)S(1)}, bf16[2,64,512]{2,1,0:T(8,128)(2,1)S(1)}, u32[]{:S(2)}, u32[]{:S(2)}) collective-permute-start(bf16[2,64,512]{2,1,0:T(8,128)(2,1)S(1)} %get-tuple-element.15), channel_id=1, source_target_pairs={{32,0},{33,1},{34,2},{35,3},{36,4},{37,5},{38,6},{39,7},{40,8},{41... | collective-permute-start | bytes 393224 | tf_op jit(solution)/shard_map/ppermute | solution.py:23
  2.3 8.1 %collective-permute-start = (bf16[2,64,512]{2,1,0:T(8,128)(2,1)S(1)}, bf16[2,64,512]{2,1,0:T(8,128)(2,1)S(1)}, u32[]{:S(2)}, u32[]{:S(2)}) collective-permute-start(bf16[2,64,512]{2,1,0:T(8,128)(2,1)S(1)} %get-tuple-element.16), channel_id=1, source_target_pairs={{0,32},{1,33},{2,34},{3,35},{4,36},{5,37},{6,38},{7,39},{8,40},{9,... | collective-permute-start | bytes 393224 | tf_op jit(solution)/shard_map/ppermute | solution.py:23
  10.4 1.2 fusion.23
  12.1 17.7 %all-reduce.3 = (f32[32]{0:T(128)S(1)}, f32[32]{0:T(128)S(1)}) all-reduce(f32[32]{0:T(128)S(1)} %reduce_sum.39, f32[32]{0:T(128)S(1)} %reduce_sum.37), channel_id=1, replica_groups=mesh['scene'=2,'view_0'=8,'view_1'=8,'view_2'=2] {'view_0'}, use_global_device_ids=true, to_apply=%region_7.8 | all-reduce | flops 64 | bytes 512 | tf_op jit(solution)/shard_map/psum | solution.py:16
  29.8 14.1 %all-reduce.2 = (f32[32]{0:T(128)S(1)}, f32[32]{0:T(128)S(1)}) all-reduce(f32[32]{0:T(128)S(1)} %get-tuple-element.9, f32[32]{0:T(128)S(1)} %get-tuple-element.10), channel_id=1, replica_groups=mesh['scene'=2,'view_0'=8,'view_1'=8,'view_2'=2] {'view_1'}, use_global_device_ids=true, to_apply=%region_8.9 | all-reduce | flops 64 | bytes 512 | tf_op jit(solution)/shard_map/psum | solution.py:16
  43.9 16.6 %all-reduce.4 = (f32[32]{0:T(128)S(1)}, f32[32]{0:T(128)S(1)}) all-reduce(f32[32]{0:T(128)S(1)} %get-tuple-element.7, f32[32]{0:T(128)S(1)} %get-tuple-element.8), channel_id=1, replica_groups=mesh['scene'=2,'view_0'=8,'view_1'=8,'view_2'=2] {'view_2'}, use_global_device_ids=true, to_apply=%region_9.10 | all-reduce | flops 64 | bytes 512 | tf_op jit(solution)/shard_map/psum | solution.py:16
  60.8 0.7 multiply_subtract_fusion
  61.6 1.2 constant_dynamic-update-slice_fusion.1
  63.4 1.6 %fusion.34 = f32[10,64,512]{2,1,0:T(8,128)S(1)} fusion(bf16[12,64,512]{2,1,0:T(8,128)(2,1)S(1)} %fusion.24, bf16[512,3,3,512]{3,0,2,1:T(8,128)(2,1)} %param.10), kind=kOutput, calls=%fused_computation.42 | convolution fusion | flops 335544320 | bytes 2621440 | tf_op jit(solution)/shard_map/rwi,oi->rwo/dot_general | solution.py:31
  68.9 0.7 fusion.25
  69.6 3.5 %broadcast_in_dim.56 = bf16[10,2,64,2,512]{4,3,2,1,0:T(2,128)(2,1)} broadcast(bf16[10,64,512]{2,1,0:T(8,128)(2,1)S(1)} %fusion.25), dimensions={0,2,4} | broadcast | bytes 3276800 | tf_op jit(solution)/shard_map/broadcast_in_dim | solution.py:90
  73.1 3.8 %reshape.41 = bf16[20,128,512]{2,1,0:T(8,128)(2,1)S(1)} reshape(bf16[10,2,64,2,512]{4,3,2,1,0:T(2,128)(2,1)} %broadcast_in_dim.56) | data formatting | bytes 5242880 | tf_op jit(solution)/shard_map/reshape | solution.py:91
  77.1 4.4 %fusion.8 = f32[16,128,512]{2,1,0:T(8,128)} fusion(bf16[18,128,512]{2,1,0:T(8,128)(2,1)S(1)} %slice.175, bf16[512,3,3,512]{3,0,2,1:T(8,128)(2,1)} %param.12), kind=kOutput, calls=%fused_computation.9 | convolution fusion | flops 1073741824 | bytes 7077888 | tf_op jit(solution)/shard_map/rwi,oi->rwo/dot_general | solution.py:31
  81.5 4.3 %fusion.6 = f32[16,128,512]{2,1,0:T(8,128)} fusion(bf16[18,128,512]{2,1,0:T(8,128)(2,1)S(1)} %slice.175, bf16[512,3,3,512]{3,0,2,1:T(8,128)(2,1)} %param.12), kind=kOutput, calls=%fused_computation.7 | convolution fusion | flops 1073741824 | bytes 7077888 | tf_op jit(solution)/shard_map/rwi,oi->rwo/dot_general | solution.py:31
  85.8 3.3 %fusion.4 = f32[16,128,512]{2,1,0:T(8,128)} fusion(bf16[18,128,512]{2,1,0:T(8,128)(2,1)S(1)} %slice.175, bf16[512,3,3,512]{3,0,2,1:T(8,128)(2,1)S(1)} %bitcast.99), kind=kOutput, calls=%fused_computation.5 | convolution fusion | flops 1073741824 | bytes 7077888 | tf_op jit(solution)/shard_map/rwi,oi->rwo/dot_general | solution.py:31
  89.1 3.3 %fusion.2 = f32[16,128,512]{2,1,0:T(8,128)} fusion(bf16[18,128,512]{2,1,0:T(8,128)(2,1)S(1)} %slice.175, bf16[512,3,3,512]{3,0,2,1:T(8,128)(2,1)S(1)} %bitcast.99), kind=kOutput, calls=%fused_computation.3 | convolution fusion | flops 1073741824 | bytes 7077888 | tf_op jit(solution)/shard_map/rwi,oi->rwo/dot_general | solution.py:31
  92.4 3.2 %fusion = f32[16,128,512]{2,1,0:T(8,128)} fusion(bf16[18,128,512]{2,1,0:T(8,128)(2,1)S(1)} %slice.175, bf16[512,3,3,512]{3,0,2,1:T(8,128)(2,1)S(1)} %bitcast.99), kind=kOutput, calls=%fused_computation.1 | convolution fusion | flops 1073741824 | bytes 7077888 | tf_op jit(solution)/shard_map/rwi,oi->rwo/dot_general | solution.py:31
  95.6 3.3 %fusion.10 = f32[16,128,512]{2,1,0:T(8,128)} fusion(bf16[18,128,512]{2,1,0:T(8,128)(2,1)S(1)} %slice.175, bf16[512,3,3,512]{3,0,2,1:T(8,128)(2,1)S(1)} %bitcast.99), kind=kOutput, calls=%fused_computation.11 | convolution fusion | flops 1073741824 | bytes 7077888 | tf_op jit(solution)/shard_map/rwi,oi->rwo/dot_general | solution.py:31
  98.9 3.3 %fusion.52 = f32[16,128,512]{2,1,0:T(8,128)} fusion(bf16[20,128,512]{2,1,0:T(8,128)(2,1)S(1)} %reshape.41, bf16[512,3,3,512]{3,0,2,1:T(8,128)(2,1)S(1)} %bitcast.99), kind=kOutput, calls=%fused_computation.60 | convolution fusion | flops 1073741824 | bytes 7340032 | tf_op jit(solution)/shard_map/rwi,oi->rwo/dot_general | solution.py:31
  102.2 2.9 %broadcast_in_dim.57 = bf16[8,2,64,2,512]{4,3,2,1,0:T(2,128)(2,1)} broadcast(bf16[8,64,512]{2,1,0:T(8,128)(2,1)S(1)} %slice-done), dimensions={0,2,4} | broadcast | bytes 2621440 | tf_op jit(solution)/shard_map/broadcast_in_dim | solution.py:90
  105.1 4.1 %slice.164 = bf16[16,128,512]{2,1,0:T(8,128)(2,1)} reshape(bf16[8,2,64,2,512]{4,3,2,1,0:T(2,128)(2,1)} %broadcast_in_dim.57) | data formatting | bytes 4194304 | tf_op jit(solution)/shard_map/slice | solution.py:30
  109.3 3.1 %fusion.48 = f32[16,128,512]{2,1,0:T(8,128)S(1)} fusion(bf16[16,128,512]{2,1,0:T(8,128)(2,1)} %slice.164, bf16[512,3,3,512]{3,0,2,1:T(8,128)(2,1)} %param.12), kind=kOutput, calls=%fused_computation.56 | convolution fusion | flops 1073741824 | bytes 6815744 | tf_op jit(solution)/shard_map/rwi,oi->rwo/dot_general | solution.py:31
  112.4 11.0 %add_convert_fusion = bf16[16,128,512]{2,1,0:T(8,128)(2,1)} fusion(f32[16,128,512]{2,1,0:T(8,128)} %fusion, f32[16,128,512]{2,1,0:T(8,128)} %fusion.2, f32[16,128,512]{2,1,0:T(8,128)} %fusion.4, f32[16,128,512]{2,1,0:T(8,128)S(1)} %fusion.48, f32[16,128,512]{2,1,0:T(8,128)} %fusion.6, f32[16,128,512]{2,1,0:T(8,128)S(1)} %copy-done, ...), kind=kOutput, calls=%fused_computation | convolution fusion | flops 1084227584 | bytes 38799360 | tf_op jit(solution)/shard_map/rwi,oi->rwo/dot_general | solution.py:31
  (41 shorter events, 5.4 us)
Async XLA Ops:
  1.0 61.8 %collective-permute-start.1 = (bf16[2,64,512]{2,1,0:T(8,128)(2,1)S(1)}, bf16[2,64,512]{2,1,0:T(8,128)(2,1)S(1)}, u32[]{:S(2)}, u32[]{:S(2)}) collective-permute-start(bf16[2,64,512]{2,1,0:T(8,128)(2,1)S(1)} %get-tuple-element.15), channel_id=1, source_target_pairs={{32,0},{33,1},{34,2},{35,3},{36,4},{37,5},{38,6},{39,7},{40,8},{41... | collective-permute-start | bytes 393224 | tf_op jit(solution)/shard_map/ppermute | solution.py:23
  2.3 59.2 %collective-permute-start = (bf16[2,64,512]{2,1,0:T(8,128)(2,1)S(1)}, bf16[2,64,512]{2,1,0:T(8,128)(2,1)S(1)}, u32[]{:S(2)}, u32[]{:S(2)}) collective-permute-start(bf16[2,64,512]{2,1,0:T(8,128)(2,1)S(1)} %get-tuple-element.16), channel_id=1, source_target_pairs={{0,32},{1,33},{2,34},{3,35},{4,36},{5,37},{6,38},{7,39},{8,40},{9,... | collective-permute-start | bytes 393224 | tf_op jit(solution)/shard_map/ppermute | solution.py:23
  61.6 3.4 %copy-start.2 = (bf16[512,3,3,512]{3,0,2,1:T(8,128)(2,1)S(1)}, bf16[512,3,3,512]{3,0,2,1:T(8,128)(2,1)}, u32[]{:S(2)}) copy-start(bf16[512,3,3,512]{3,0,2,1:T(8,128)(2,1)} %param.10) | copy-start | bytes 14155780
  68.2 0.7 copy-start.3
  69.6 7.3 %copy-start.1 = (bf16[10,64,512]{2,1,0:T(8,128)(2,1)}, bf16[10,64,512]{2,1,0:T(8,128)(2,1)S(1)}, u32[]{:S(2)}) copy-start(bf16[10,64,512]{2,1,0:T(8,128)(2,1)S(1)} %fusion.25) | copy-start | bytes 1966084
  76.9 8.9 %slice-start.1 = ((s8[4718592]{0:T(1024)(128)(4,1)}), s8[4194304]{0:T(1024)(128)(4,1)S(1)}, s32[]{:S(2)}) async-start(s8[4718592]{0:T(1024)(128)(4,1)} %bitcast.98), calls=%async_computation.1 | async-start | bytes 8388608
  77.1 8.8 %slice-start.2 = ((s8[4718592]{0:T(1024)(128)(4,1)}), s8[524288]{0:T(1024)(128)(4,1)S(1)}, s32[]{:S(2)}) async-start(s8[4718592]{0:T(1024)(128)(4,1)} %bitcast.98), calls=%async_computation.2 | async-start | bytes 1048576
  98.9 3.3 %slice-start = ((bf16[10,64,512]{2,1,0:T(8,128)(2,1)}), bf16[8,64,512]{2,1,0:T(8,128)(2,1)S(1)}, s32[]{:S(2)}) async-start(bf16[10,64,512]{2,1,0:T(8,128)(2,1)} %copy-done.1), calls=%async_computation | async-start | bytes 1048576 | tf_op jit(solution)/shard_map/slice | solution.py:30
  109.3 3.1 %copy-start = (f32[16,128,512]{2,1,0:T(8,128)S(1)}, f32[16,128,512]{2,1,0:T(8,128)}, u32[]{:S(2)}) copy-start(f32[16,128,512]{2,1,0:T(8,128)} %fusion.8) | copy-start | bytes 12582916
  109.3 3.1 %copy-start.4 = (f32[512]{0:T(512)S(1)}, f32[512]{0:T(512)}, u32[]{:S(2)}) copy-start(f32[512]{0:T(512)} %param.13) | copy-start | bytes 6148
where the time goes:
time: 124 us; the launch traced here: 123 us
  blocking collectives  48.4 us (39%)
  matrix products  45.2 us (36%)
  local copies, waits for them, and re-layouts  17.3 us (14%)
  starting transfers between devices  9.42 us (8%)
  other arithmetic  2.69 us (2%)
    psum x3, blocking collectives, one_axis_at_a_time(): array = lax.psum(array, axis)  48.4 us
    dot_general x18, matrix products, conv_taps(): jnp.einsum('rwi,oi->rwo', window, filters[:, tap_row, tap_col, :], prefer...  45.2 us
    ppermute x2, starting transfers between devices, shifted(): return lax.ppermute(block, axis, route)  9.42 us
    broadcast_in_dim x2, local copies, waits for them, and re-layouts, per_device(): jnp.broadcast_to(mixed[:, None, :, None, :], (tall_rows, 2, columns, 2, c...  6.44 us
    slice x3, local copies, waits for them, and re-layouts, conv_taps(): window = padded[tap_row:tap_row + out_rows, tap_col:tap_col + out_cols, :]  4.14 us
    reshape x1, local copies, waits for them, and re-layouts, per_device(): doubled = doubled.reshape(2 * tall_rows, 2 * columns, channels)  3.75 us
  transfers between devices with their start and end apart: 2, of which 0 were waited for; matrix products, arithmetic and copies ran while one was open for 3% of the time, Pallas kernels for 0%

commit v1 on v0

--- a/solution.py
+++ b/solution.py
@@ -11,9 +11,15 @@
 epsilon = 1e-06
 
 
+def add_all(shard, name):
+    parts = lax.all_gather(shard, name, axis=0, tiled=False)
+    total = parts.sum(axis=0)
+    return total
+
+
 def one_axis_at_a_time(array, axes):
     for axis in axes:
-        array = lax.psum(array, axis)
+        array = add_all(array, axis)
     return array
 
 

time: 124 us -> 132 us (1.065)
  local copies, waits for them, and re-layouts: 17.3 us -> 23 us
  between operations: 0.26 us -> 2.17 us
    psum x3 -> x0, blocking collectives: 48.4 us -> none  [one_axis_at_a_time(): array = lax.psum(array, axis)]
    unnamed x0 -> x3, blocking collectives: none -> 48.3 us
    unnamed x16 -> x31, local copies, waits for them, and re-layouts: 1.4 us -> 6.54 us
  transfers between devices with their start and end apart: 2 -> 2, of which waited for: 0 -> 0; matrix products, arithmetic and copies ran while one was open for 3% -> 7% of each run, Pallas kernels for 0% -> 0%
where the time goes in v1:
time: 132 us; the launch traced here: 131 us
  blocking collectives  48.3 us (37%)
  matrix products  45.2 us (34%)
  local copies, waits for them, and re-layouts  23 us (17%)
  starting transfers between devices  9.42 us (7%)
  other arithmetic  2.81 us (2%)
  between operations  2.17 us (2%)
    unnamed x3, blocking collectives  48.3 us
    dot_general x18, matrix products, conv_taps(): jnp.einsum('rwi,oi->rwo', window, filters[:, tap_row, tap_col, :], prefer...  45.2 us
    ppermute x2, starting transfers between devices, shifted(): return lax.ppermute(block, axis, route)  9.42 us
    unnamed x31, local copies, waits for them, and re-layouts  6.54 us
    broadcast_in_dim x2, local copies, waits for them, and re-layouts, per_device(): jnp.broadcast_to(mixed[:, None, :, None, :], (tall_rows, 2, columns, 2, c...  6.44 us
    slice x3, local copies, waits for them, and re-layouts, conv_taps(): window = padded[tap_row:tap_row + out_rows, tap_col:tap_col + out_cols, :]  4.14 us
    reshape x1, local copies, waits for them, and re-layouts, per_device(): doubled = doubled.reshape(2 * tall_rows, 2 * columns, channels)  3.75 us
  transfers between devices with their start and end apart: 2, of which 0 were waited for; matrix products, arithmetic and copies ran while one was open for 7% of the time, Pallas kernels for 0%

profile of v1, /device:TPU:513, one launch (start us, length us, event | category | flops | bytes accessed | tf_op | source)
XLA Modules:
  0.0 130.9 jit_solution(5807273469263583007)
XLA Ops:
  1.0 1.3 collective-permute-start.1
  2.3 8.1 %collective-permute-start = (bf16[2,64,512]{2,1,0:T(8,128)(2,1)S(1)}, bf16[2,64,512]{2,1,0:T(8,128)(2,1)S(1)}, u32[]{:S(2)}, u32[]{:S(2)}) collective-permute-start(bf16[2,64,512]{2,1,0:T(8,128)(2,1)S(1)} %get-tuple-element.16), channel_id=1, source_target_pairs={{0,32},{1,33},{2,34},{3,35},{4,36},{5,37},{6,38},{7,39},{8,40},{9,... | collective-permute-start | bytes 393224 | tf_op jit(solution)/shard_map/ppermute | solution.py:29
  10.4 1.2 fusion.23
  11.7 1.3 dynamic-slice.2
  12.9 1.3 dynamic-slice.1
  15.4 1.3 dynamic-slice
  18.2 17.0 %all-reduce.9 = (f32[256]{0:T(256)S(1)}, f32[256]{0:T(256)S(1)}) all-reduce(f32[256]{0:T(256)S(1)} %dynamic-update-slice.3, f32[256]{0:T(256)S(1)} %dynamic-update-slice), channel_id=5, replica_groups=mesh['scene'=2,'view_0'=8,'view_1'=8,'view_2'=2] {'view_0'}, use_global_device_ids=true, to_apply=%add.5 | all-reduce | flops 512 | bytes 4096
  35.8 14.2 %all-reduce.8 = (f32[256]{0:T(256)S(1)}, f32[256]{0:T(256)S(1)}) all-reduce(f32[256]{0:T(256)S(1)} %dynamic-update-slice.4, f32[256]{0:T(256)S(1)} %dynamic-update-slice.1), channel_id=6, replica_groups=mesh['scene'=2,'view_0'=8,'view_1'=8,'view_2'=2] {'view_1'}, use_global_device_ids=true, to_apply=%add.6 | all-reduce | flops 512 | bytes 4096
  50.7 17.2 %all-reduce.10 = (f32[64]{0:T(128)S(1)}, f32[64]{0:T(128)S(1)}) all-reduce(f32[64]{0:T(128)S(1)} %dynamic-update-slice.5, f32[64]{0:T(128)S(1)} %dynamic-update-slice.2), channel_id=7, replica_groups=mesh['scene'=2,'view_0'=8,'view_1'=8,'view_2'=2] {'view_2'}, use_global_device_ids=true, to_apply=%add.7 | all-reduce | flops 128 | bytes 1024
  69.1 1.2 constant_dynamic-update-slice_fusion.1
  70.9 1.6 %fusion.34 = f32[10,64,512]{2,1,0:T(8,128)S(1)} fusion(bf16[12,64,512]{2,1,0:T(8,128)(2,1)S(1)} %fusion.24, bf16[512,3,3,512]{3,0,2,1:T(8,128)(2,1)} %param.10), kind=kOutput, calls=%fused_computation.42 | convolution fusion | flops 335544320 | bytes 2621440 | tf_op jit(solution)/shard_map/rwi,oi->rwo/dot_general | solution.py:37
  77.2 3.5 %broadcast_in_dim.56 = bf16[10,2,64,2,512]{4,3,2,1,0:T(2,128)(2,1)} broadcast(bf16[10,64,512]{2,1,0:T(8,128)(2,1)S(1)} %fusion.25), dimensions={0,2,4} | broadcast | bytes 3276800 | tf_op jit(solution)/shard_map/broadcast_in_dim | solution.py:96
  80.7 3.8 %reshape.51 = bf16[20,128,512]{2,1,0:T(8,128)(2,1)S(1)} reshape(bf16[10,2,64,2,512]{4,3,2,1,0:T(2,128)(2,1)} %broadcast_in_dim.56) | data formatting | bytes 5242880 | tf_op jit(solution)/shard_map/reshape | solution.py:97
  84.6 4.4 %fusion.8 = f32[16,128,512]{2,1,0:T(8,128)} fusion(bf16[18,128,512]{2,1,0:T(8,128)(2,1)S(1)} %slice.175, bf16[512,3,3,512]{3,0,2,1:T(8,128)(2,1)} %param.12), kind=kOutput, calls=%fused_computation.9 | convolution fusion | flops 1073741824 | bytes 7077888 | tf_op jit(solution)/shard_map/rwi,oi->rwo/dot_general | solution.py:37
  89.0 4.3 %fusion.6 = f32[16,128,512]{2,1,0:T(8,128)} fusion(bf16[18,128,512]{2,1,0:T(8,128)(2,1)S(1)} %slice.175, bf16[512,3,3,512]{3,0,2,1:T(8,128)(2,1)} %param.12), kind=kOutput, calls=%fused_computation.7 | convolution fusion | flops 1073741824 | bytes 7077888 | tf_op jit(solution)/shard_map/rwi,oi->rwo/dot_general | solution.py:37
  93.4 3.3 %fusion.4 = f32[16,128,512]{2,1,0:T(8,128)} fusion(bf16[18,128,512]{2,1,0:T(8,128)(2,1)S(1)} %slice.175, bf16[512,3,3,512]{3,0,2,1:T(8,128)(2,1)S(1)} %bitcast.102), kind=kOutput, calls=%fused_computation.5 | convolution fusion | flops 1073741824 | bytes 7077888 | tf_op jit(solution)/shard_map/rwi,oi->rwo/dot_general | solution.py:37
  96.7 3.3 %fusion.2 = f32[16,128,512]{2,1,0:T(8,128)} fusion(bf16[18,128,512]{2,1,0:T(8,128)(2,1)S(1)} %slice.175, bf16[512,3,3,512]{3,0,2,1:T(8,128)(2,1)S(1)} %bitcast.102), kind=kOutput, calls=%fused_computation.3 | convolution fusion | flops 1073741824 | bytes 7077888 | tf_op jit(solution)/shard_map/rwi,oi->rwo/dot_general | solution.py:37
  99.9 3.2 %fusion = f32[16,128,512]{2,1,0:T(8,128)} fusion(bf16[18,128,512]{2,1,0:T(8,128)(2,1)S(1)} %slice.175, bf16[512,3,3,512]{3,0,2,1:T(8,128)(2,1)S(1)} %bitcast.102), kind=kOutput, calls=%fused_computation.1 | convolution fusion | flops 1073741824 | bytes 7077888 | tf_op jit(solution)/shard_map/rwi,oi->rwo/dot_general | solution.py:37
  103.2 3.3 %fusion.10 = f32[16,128,512]{2,1,0:T(8,128)} fusion(bf16[18,128,512]{2,1,0:T(8,128)(2,1)S(1)} %slice.175, bf16[512,3,3,512]{3,0,2,1:T(8,128)(2,1)S(1)} %bitcast.102), kind=kOutput, calls=%fused_computation.11 | convolution fusion | flops 1073741824 | bytes 7077888 | tf_op jit(solution)/shard_map/rwi,oi->rwo/dot_general | solution.py:37
  106.5 3.3 %fusion.52 = f32[16,128,512]{2,1,0:T(8,128)} fusion(bf16[20,128,512]{2,1,0:T(8,128)(2,1)S(1)} %reshape.51, bf16[512,3,3,512]{3,0,2,1:T(8,128)(2,1)S(1)} %bitcast.102), kind=kOutput, calls=%fused_computation.60 | convolution fusion | flops 1073741824 | bytes 7340032 | tf_op jit(solution)/shard_map/rwi,oi->rwo/dot_general | solution.py:37
  109.7 2.9 %broadcast_in_dim.57 = bf16[8,2,64,2,512]{4,3,2,1,0:T(2,128)(2,1)} broadcast(bf16[8,64,512]{2,1,0:T(8,128)(2,1)S(1)} %slice-done), dimensions={0,2,4} | broadcast | bytes 2621440 | tf_op jit(solution)/shard_map/broadcast_in_dim | solution.py:96
  112.7 4.1 %slice.164 = bf16[16,128,512]{2,1,0:T(8,128)(2,1)} reshape(bf16[8,2,64,2,512]{4,3,2,1,0:T(2,128)(2,1)} %broadcast_in_dim.57) | data formatting | bytes 4194304 | tf_op jit(solution)/shard_map/slice | solution.py:36
  116.8 3.1 %fusion.48 = f32[16,128,512]{2,1,0:T(8,128)S(1)} fusion(bf16[16,128,512]{2,1,0:T(8,128)(2,1)} %slice.164, bf16[512,3,3,512]{3,0,2,1:T(8,128)(2,1)} %param.12), kind=kOutput, calls=%fused_computation.56 | convolution fusion | flops 1073741824 | bytes 6815744 | tf_op jit(solution)/shard_map/rwi,oi->rwo/dot_general | solution.py:37
  119.9 11.0 %add_convert_fusion = bf16[16,128,512]{2,1,0:T(8,128)(2,1)} fusion(f32[16,128,512]{2,1,0:T(8,128)} %fusion, f32[16,128,512]{2,1,0:T(8,128)} %fusion.2, f32[16,128,512]{2,1,0:T(8,128)} %fusion.4, f32[16,128,512]{2,1,0:T(8,128)S(1)} %fusion.48, f32[16,128,512]{2,1,0:T(8,128)} %fusion.6, f32[16,128,512]{2,1,0:T(8,128)S(1)} %copy-done, ...), kind=kOutput, calls=%fused_computation | convolution fusion | flops 1084227584 | bytes 38799360 | tf_op jit(solution)/shard_map/rwi,oi->rwo/dot_general | solution.py:37
  (68 shorter events, 9.7 us)
Async XLA Ops:
  1.0 69.4 %collective-permute-start.1 = (bf16[2,64,512]{2,1,0:T(8,128)(2,1)S(1)}, bf16[2,64,512]{2,1,0:T(8,128)(2,1)S(1)}, u32[]{:S(2)}, u32[]{:S(2)}) collective-permute-start(bf16[2,64,512]{2,1,0:T(8,128)(2,1)S(1)} %get-tuple-element.15), channel_id=1, source_target_pairs={{32,0},{33,1},{34,2},{35,3},{36,4},{37,5},{38,6},{39,7},{40,8},{41... | collective-permute-start | bytes 393224 | tf_op jit(solution)/shard_map/ppermute | solution.py:29
  2.3 66.8 %collective-permute-start = (bf16[2,64,512]{2,1,0:T(8,128)(2,1)S(1)}, bf16[2,64,512]{2,1,0:T(8,128)(2,1)S(1)}, u32[]{:S(2)}, u32[]{:S(2)}) collective-permute-start(bf16[2,64,512]{2,1,0:T(8,128)(2,1)S(1)} %get-tuple-element.16), channel_id=1, source_target_pairs={{0,32},{1,33},{2,34},{3,35},{4,36},{5,37},{6,38},{7,39},{8,40},{9,... | collective-permute-start | bytes 393224 | tf_op jit(solution)/shard_map/ppermute | solution.py:29
  69.1 3.4 %copy-start.2 = (bf16[512,3,3,512]{3,0,2,1:T(8,128)(2,1)S(1)}, bf16[512,3,3,512]{3,0,2,1:T(8,128)(2,1)}, u32[]{:S(2)}) copy-start(bf16[512,3,3,512]{3,0,2,1:T(8,128)(2,1)} %param.10) | copy-start | bytes 14155780
  75.8 0.7 copy-start.3
  77.2 7.3 %copy-start.1 = (bf16[10,64,512]{2,1,0:T(8,128)(2,1)}, bf16[10,64,512]{2,1,0:T(8,128)(2,1)S(1)}, u32[]{:S(2)}) copy-start(bf16[10,64,512]{2,1,0:T(8,128)(2,1)S(1)} %fusion.25) | copy-start | bytes 1966084
  84.4 8.9 %slice-start.1 = ((s8[4718592]{0:T(1024)(128)(4,1)}), s8[4194304]{0:T(1024)(128)(4,1)S(1)}, s32[]{:S(2)}) async-start(s8[4718592]{0:T(1024)(128)(4,1)} %bitcast.101), calls=%async_computation.1 | async-start | bytes 8388608
  84.6 8.8 %slice-start.2 = ((s8[4718592]{0:T(1024)(128)(4,1)}), s8[524288]{0:T(1024)(128)(4,1)S(1)}, s32[]{:S(2)}) async-start(s8[4718592]{0:T(1024)(128)(4,1)} %bitcast.101), calls=%async_computation.2 | async-start | bytes 1048576
  106.5 3.3 %slice-start = ((bf16[10,64,512]{2,1,0:T(8,128)(2,1)}), bf16[8,64,512]{2,1,0:T(8,128)(2,1)S(1)}, s32[]{:S(2)}) async-start(bf16[10,64,512]{2,1,0:T(8,128)(2,1)} %copy-done.1), calls=%async_computation | async-start | bytes 1048576 | tf_op jit(solution)/shard_map/slice | solution.py:36
  116.8 3.1 %copy-start = (f32[16,128,512]{2,1,0:T(8,128)S(1)}, f32[16,128,512]{2,1,0:T(8,128)}, u32[]{:S(2)}) copy-start(f32[16,128,512]{2,1,0:T(8,128)} %fusion.8) | copy-start | bytes 12582916
  116.8 3.1 %copy-start.4 = (f32[512]{0:T(512)S(1)}, f32[512]{0:T(512)}, u32[]{:S(2)}) copy-start(f32[512]{0:T(512)} %param.13) | copy-start | bytes 6148
